TPU v7x, 32 devices: a whole 2x2x4 slice. The times are simulated.
32 devices in a mesh: member: 4 (over x, core), region: 8 (over z, y).
Axes of the slice: x: 2, y: 2, z: 4, core: 2. Of those that a mesh axis runs over, the one named last changes fastest.
Arguments:
- ensemble: float32 [12, 16, 32, 512], P('member', 'region'), may hold values from -6 to 6
- obs_value: float32 [16, 32, 128], P(None, ('member', 'region')), may hold values from -6 to 6
- obs_error: float32 [16, 32, 128], P(None, ('member', 'region')), may hold values from 0.5 to 4
- obs_index: int32 [16, 32, 128], P(None, ('member', 'region')), may hold values from 0 to 511
- obs_count: int32 [16, 32], P(None, ('member', 'region')), may hold values from 1 to 128
Outputs:
- analysis: float32 [12, 16, 32, 512], P('member', 'region')
Inputs may be any that keep to these rules, and one draw needn't show every extreme that they name: `obs_index`: value v names field v // (256) (0 SST, 1 SSH) at cell v mod (256) of the block, cells row-major. `obs_count`: slots below a block's count are observations; the others are padding and carry no weight.
All inputs are finite; a program needn't handle non-finite values.
Results may differ from a plain program's by a relative error of at most 0.0001.
Values sent between devices are 32-bit elements; how exact they have to be, the bound alone decides.
A program may use at most 64 MiB of HBM per device.

v0:
```python
import math
import jax
import jax.numpy as jnp
from jax import lax
from jax.sharding import PartitionSpec as P

SIDE = 16
NS_ITERS = 6
LOC_SCALE = 12.0
INFLATION_FACTOR = 1.1


def padded_2(cells, sides, width):
    for axis, dim in sides:
        count = lax.axis_size(axis)
        ends = count - 1
        head = lax.slice_in_dim(cells, 0, width, axis=dim)
        tail = lax.slice_in_dim(cells, cells.shape[dim] - width, cells.shape[dim], axis=dim)
        cells = jnp.concatenate(
            [
                lax.ppermute(tail, axis, [(i, (i + 1) % count) for i in range(ends)]),
                cells,
                lax.ppermute(head, axis, [((i + 1) % count, i) for i in range(ends)]),
            ],
            axis=dim,
        )
    return cells


def batch_product(left, right):
    return jnp.einsum("...ij,...jk->...ik", left, right, precision=lax.Precision.HIGHEST)


def observe(ensemble, obs_value, obs_error, obs_index, obs_count):
    ens_mean = jnp.mean(ensemble, axis=0)
    anomaly = ensemble - ens_mean
    slot_index = lax.broadcasted_iota(jnp.int32, obs_index.shape, 2)
    live_slot = jnp.where(slot_index < obs_count[:, :, None], 1.0, 0.0).astype(jnp.float32)
    root_weight = jnp.sqrt(live_slot / obs_error)
    value_count = anomaly.shape[3]
    value_ids = lax.broadcasted_iota(jnp.int32, (1, 1, 1, value_count), 3)
    selector = jnp.where(obs_index[:, :, :, None] == value_ids, 1.0, 0.0).astype(jnp.float32)
    seen_anom = jnp.einsum("rcov,krcv->rcko", selector, anomaly, precision=lax.Precision.HIGHEST)
    seen_mean = jnp.einsum("rcov,rcv->rco", selector, ens_mean, precision=lax.Precision.HIGHEST)
    rescaled_values = root_weight[:, :, None] * seen_anom
    innovation = root_weight * (obs_value - seen_mean)
    cell_index = obs_index % (SIDE * SIDE)
    rowpos = (cell_index // SIDE).astype(jnp.float32)
    column_position = (cell_index % SIDE).astype(jnp.float32)
    stacked = jnp.concatenate(
        [rescaled_values, innovation[:, :, None], rowpos[:, :, None], column_position[:, :, None]],
        axis=2,
    )
    return (anomaly, ens_mean, stacked)


def analyze(anomaly, ens_mean, padded):
    ensemble_members = anomaly.shape[0]
    row_count = anomaly.shape[1]
    col_count = anomaly.shape[2]
    pieces = []
    for row_step in range(3):
        for col_step in range(3):
            pieces.append(padded[row_step : row_step + row_count, col_step : col_step + col_count])
    nearby = jnp.stack(pieces, axis=2)
    rescaled_values = nearby[:, :, :, :ensemble_members]
    innovation = nearby[:, :, :, ensemble_members]
    rowpos = nearby[:, :, :, ensemble_members + 1]
    column_position = nearby[:, :, :, ensemble_members + 2]
    offset_index = jnp.arange(9, dtype=jnp.int32)
    offset_row = (offset_index // 3 - 1).astype(jnp.float32) * SIDE
    offset_col = (offset_index % 3 - 1).astype(jnp.float32) * SIDE
    half_side = SIDE // 2
    point_index = jnp.arange(4, dtype=jnp.int32)
    center_row = (point_index // 2).astype(jnp.float32) * half_side + (half_side - 1) * 0.5
    center_col = (point_index % 2).astype(jnp.float32) * half_side + (half_side - 1) * 0.5
    row_gap = offset_row[:, None] + rowpos
    col_gap = offset_col[:, None] + column_position
    distance = (row_gap[:, :, None] - center_row[:, None, None]) ** 2 + (
        col_gap[:, :, None] - center_col[:, None, None]
    ) ** 2
    locality = jnp.exp(-distance / (2.0 * LOC_SCALE * LOC_SCALE))
    weighted = locality[:, :, :, :, None, :] * rescaled_values[:, :, None]
    gramian_total = jnp.einsum(
        "rcpnko,rcnjo->rcpkj", weighted, rescaled_values, precision=lax.Precision.HIGHEST
    )
    drive_vec = jnp.einsum(
        "rcpnko,rcno->rcpk", weighted, innovation, precision=lax.Precision.HIGHEST
    )
    identity_matrix = jnp.eye(ensemble_members, dtype=jnp.float32)
    precision_matrix = gramian_total + (ensemble_members - 1) / INFLATION_FACTOR * identity_matrix
    norm_scale = jnp.sqrt(jnp.sum(precision_matrix * precision_matrix, axis=(3, 4), keepdims=True))
    root_iter = precision_matrix / norm_scale
    inv_iter = jnp.broadcast_to(identity_matrix, precision_matrix.shape)
    for sweep_index in range(NS_ITERS):
        ns_step = 1.5 * identity_matrix - 0.5 * batch_product(inv_iter, root_iter)
        root_iter = batch_product(root_iter, ns_step)
        inv_iter = batch_product(ns_step, inv_iter)
    inv_root = inv_iter / jnp.sqrt(norm_scale)
    half_way = jnp.einsum("rcpkj,rcpj->rcpk", inv_root, drive_vec, precision=lax.Precision.HIGHEST)
    mean_w = jnp.einsum("rcpkj,rcpj->rcpk", inv_root, half_way, precision=lax.Precision.HIGHEST)
    weights = mean_w[..., :, None] + math.sqrt(ensemble_members - 1) * inv_root
    point_weights = weights.reshape(row_count, col_count, 2, 2, ensemble_members, ensemble_members)
    shaped = anomaly.reshape(ensemble_members, row_count, col_count, 2, 2, half_side, 2, half_side)
    updated = jnp.einsum(
        "jrcvaybx,rcabjk->krcvaybx", shaped, point_weights, precision=lax.Precision.HIGHEST
    )
    return ens_mean[None] + updated.reshape(anomaly.shape)


def local(ensemble, obs_value, obs_error, obs_index, obs_count):
    members_dev = ensemble.shape[0]
    rows_dev = ensemble.shape[1]
    values_len = ensemble.shape[3]
    member_count = lax.axis_size("member")
    region_count = lax.axis_size("region")
    arrived = lax.all_to_all(
        ensemble[None], ("member", "region"), split_axis=3, concat_axis=0, tiled=True
    )
    col_dev = arrived.shape[3]
    grouped = arrived.reshape(
        member_count, region_count, members_dev, rows_dev, col_dev, values_len
    )
    by_block = jnp.transpose(grouped, (0, 2, 1, 3, 4, 5)).reshape(
        member_count * members_dev, region_count * rows_dev, col_dev, values_len
    )
    anomaly, ens_mean, stacked = observe(by_block, obs_value, obs_error, obs_index, obs_count)
    with_halo = padded_2(stacked, ((("member", "region"), 1),), 1)
    padded = jnp.pad(with_halo, ((1, 1), (0, 0), (0, 0), (0, 0)))
    row_span = anomaly.shape[1] // 8

    def one_group(turn_index, result):
        first_row_index = turn_index * row_span
        part_anom = lax.dynamic_slice_in_dim(anomaly, first_row_index, row_span, 1)
        part_mean = lax.dynamic_slice_in_dim(ens_mean, first_row_index, row_span, 0)
        part_pad = lax.dynamic_slice_in_dim(padded, first_row_index, row_span + 2, 0)
        return lax.dynamic_update_slice_in_dim(
            result, analyze(part_anom, part_mean, part_pad), first_row_index, 1
        )

    result = lax.fori_loop(0, 8, one_group, jnp.zeros_like(anomaly))
    col_dev = result.shape[2]
    regrouped = result.reshape(
        member_count, members_dev, region_count, rows_dev, col_dev, values_len
    )
    outgoing = jnp.transpose(regrouped, (0, 2, 1, 3, 4, 5)).reshape(
        member_count * region_count, members_dev, rows_dev, col_dev, values_len
    )
    returned = lax.all_to_all(
        outgoing, ("member", "region"), split_axis=0, concat_axis=3, tiled=True
    )
    return returned[0]


def solution(mesh):
    return jax.shard_map(
        local,
        mesh=mesh,
        in_specs=(
            P("member", "region", None, None),
            P(None, ("member", "region"), None),
            P(None, ("member", "region"), None),
            P(None, ("member", "region"), None),
            P(None, ("member", "region")),
        ),
        out_specs=P("member", "region", None, None),
        check_vma=False,
    )
```

profile of v0, /device:TPU:0, one launch (start us, length us, event | category | flops | bytes accessed | tf_op | source)
XLA Modules:
  0.0 172.5 jit_solution(10879895825682611400)
XLA Ops:
  0.0 2.1 %copy.99 = f32[3,2,32,512]{3,1,0,2:T(2,128)} copy(f32[3,2,32,512]{3,2,1,0:T(8,128)} %param.7) | data formatting | bytes 786432 | tf_op args[0]
  2.1 7.3 %all-to-all-start = ((f32[1,3,2,32,512]{4,2,1,0,3:T(2,128)}), f32[1,3,2,32,512]{4,2,1,0,3:T(2,128)S(1)}, u32[]{:S(2)}, u32[]{:S(2)}) async-start(f32[1,3,2,32,512]{4,2,1,0,3:T(2,128)} %bitcast.189), calls=%async_computation | async-start | bytes 786432 | tf_op jit(solution)/shard_map/all_to_all | solution.py:117
  9.4 13.4 %all-to-all-done = f32[1,3,2,32,512]{4,2,1,0,3:T(2,128)S(1)} async-done(((f32[1,3,2,32,512]{4,2,1,0,3:T(2,128)}), f32[1,3,2,32,512]{4,2,1,0,3:T(2,128)S(1)}, u32[]{:S(2)}, u32[]{:S(2)}) %all-to-all-start) | async-done | bytes 393248 | tf_op jit(solution)/shard_map/all_to_all | solution.py:117
  23.4 4.1 %fusion.36 = f32[16,1,128]{2,1,0:T(1,128)S(1)} fusion(f32[16,512,1]{1,2,0:T(1,128)S(1)} %reshape.524, s32[16,128]{1,0:T(8,128)S(1)} %bitcast.316), kind=kOutput, calls=%fused_computation.88 | convolution fusion | flops 14680064 | bytes 49152 | tf_op jit(solution)/shard_map/rcov,rcv->rco/dot_general | solution.py:44
  27.6 4.0 %fusion.49 = f32[16,1,12,128]{3,2,0,1:T(8,128)S(1)} fusion(s32[16,128]{1,0:T(8,128)S(1)} %bitcast.317, f32[12,16,512]{2,1,0:T(8,128)S(1)} %broadcast_subtract_fusion.1, f32[16,128]{1,0:T(8,128)S(1)} %get-tuple-element.195), kind=kOutput, calls=%fused_computation.100 | convolution fusion | flops 153116672 | bytes 507904 | tf_op jit(solution)/shard_map/rcov,krcv->rcko/dot_general | solution.py:43
  31.6 2.9 %collective-permute-start = (f32[16,1,15,128]{3,2,0,1:T(8,128)S(1)}, f32[16,1,15,128]{3,2,0,1:T(8,128)S(1)}, u32[]{:S(2)}, u32[]{:S(2)}) collective-permute-start(f32[16,1,15,128]{3,2,0,1:T(8,128)S(1)} %pad_maximum_fusion), channel_id=1, source_target_pairs={{0,1},{1,2},{2,3},{3,4},{4,5},{5,6},{6,7},{7,8},{8,9},{9,10},{10,1... | collective-permute-start | bytes 368648 | tf_op jit(solution)/shard_map/ppermute | solution.py:21
  34.5 1.5 collective-permute-start.1
  37.5 5.5 %collective-permute-done.1 = f32[16,1,15,128]{3,2,0,1:T(8,128)S(1)} collective-permute-done((f32[16,1,15,128]{3,2,0,1:T(8,128)S(1)}, f32[16,1,15,128]{3,2,0,1:T(8,128)S(1)}, u32[]{:S(2)}, u32[]{:S(2)}) %collective-permute-start.1) | collective-permute-done | bytes 122912 | tf_op jit(solution)/shard_map/ppermute | solution.py:23
  43.2 109.6 %while.16 = (s32[]{:T(128)}, f32[12,16,1,512]{3,1,0,2:T(8,128)S(1)}, f32[16,1,512]{2,0,1:T(8,128)S(1)}, f32[18,3,15,128]{3,2,0,1:T(8,128)S(1)}, f32[12,16,1,512]...) while((s32[]{:T(128)}, ...), condition=%wide.region_3.4_spmd, body=%wide.region_1.3_spmd.sunk | while | flops 22196300 | bytes 2025700 | solution.py:141
  43.7 2.4 %convolution_bitcast_fusion.7 = f32[2,4,12,1]{2,3,1,0:T(1,128)S(1)} fusion(f32[2,9,12,128]{3,2,1,0:T(8,128)S(1)} %slice_bitcast_fusion.2, f32[2,4,9,128]{3,2,1,0:T(8,128)S(1)} %multiply_exponential_fusion.2, f32[2,9,128,1,1]{2,0,1,3,4:T(2,128)S(1)} %bitcast.308), kind=kOutput, calls=%fused_computation.17.clone.1 | convolution fusion | flops 1437696 | bytes 157056 | tf_op jit(solution)/shard_map/while/body/eval_jaxpr/rcpnko,rcno->rcpk/dot_general | solution.py:87
  52.2 2.1 %convolution_bitcast_fusion.9 = f32[12,2,1,2,2,8,2,8]{0,7,5,3,6,4,1,2:T(8,128)S(1)} fusion(f32[2,2,2,12,12,1,1]{4,3,6,5,2,1,0:T(8,128)S(1)} %bitcast.300, f32[12,2,2,2,8,2,8]{6,5,4,3,2,1,0:T(2,128)S(1)} %reshape.527), kind=kOutput, calls=%fused_computation.clone.1 | convolution fusion | flops 1769472 | bytes 102912 | tf_op jit(solution)/shard_map/while/body/eval_jaxpr/jrcvaybx,rcabjk->krcvaybx/dot_general | solution.py:105
  54.3 1.4 copy.115
  57.4 2.4 %convolution_bitcast_fusion.7 = f32[2,4,12,1]{2,3,1,0:T(1,128)S(1)} fusion(f32[2,9,12,128]{3,2,1,0:T(8,128)S(1)} %slice_bitcast_fusion.2, f32[2,4,9,128]{3,2,1,0:T(8,128)S(1)} %multiply_exponential_fusion.2, f32[2,9,128,1,1]{2,0,1,3,4:T(2,128)S(1)} %bitcast.308), kind=kOutput, calls=%fused_computation.17.clone.1 | convolution fusion | flops 1437696 | bytes 157056 | tf_op jit(solution)/shard_map/while/body/eval_jaxpr/rcpnko,rcno->rcpk/dot_general | solution.py:87
  65.9 2.1 %convolution_bitcast_fusion.9 = f32[12,2,1,2,2,8,2,8]{0,7,5,3,6,4,1,2:T(8,128)S(1)} fusion(f32[2,2,2,12,12,1,1]{4,3,6,5,2,1,0:T(8,128)S(1)} %bitcast.300, f32[12,2,2,2,8,2,8]{6,5,4,3,2,1,0:T(2,128)S(1)} %reshape.527), kind=kOutput, calls=%fused_computation.clone.1 | convolution fusion | flops 1769472 | bytes 102912 | tf_op jit(solution)/shard_map/while/body/eval_jaxpr/jrcvaybx,rcabjk->krcvaybx/dot_general | solution.py:105
  68.0 1.4 copy.115
  71.1 2.4 %convolution_bitcast_fusion.7 = f32[2,4,12,1]{2,3,1,0:T(1,128)S(1)} fusion(f32[2,9,12,128]{3,2,1,0:T(8,128)S(1)} %slice_bitcast_fusion.2, f32[2,4,9,128]{3,2,1,0:T(8,128)S(1)} %multiply_exponential_fusion.2, f32[2,9,128,1,1]{2,0,1,3,4:T(2,128)S(1)} %bitcast.308), kind=kOutput, calls=%fused_computation.17.clone.1 | convolution fusion | flops 1437696 | bytes 157056 | tf_op jit(solution)/shard_map/while/body/eval_jaxpr/rcpnko,rcno->rcpk/dot_general | solution.py:87
  79.6 2.1 %convolution_bitcast_fusion.9 = f32[12,2,1,2,2,8,2,8]{0,7,5,3,6,4,1,2:T(8,128)S(1)} fusion(f32[2,2,2,12,12,1,1]{4,3,6,5,2,1,0:T(8,128)S(1)} %bitcast.300, f32[12,2,2,2,8,2,8]{6,5,4,3,2,1,0:T(2,128)S(1)} %reshape.527), kind=kOutput, calls=%fused_computation.clone.1 | convolution fusion | flops 1769472 | bytes 102912 | tf_op jit(solution)/shard_map/while/body/eval_jaxpr/jrcvaybx,rcabjk->krcvaybx/dot_general | solution.py:105
  81.7 1.4 copy.115
  84.8 2.4 %convolution_bitcast_fusion.7 = f32[2,4,12,1]{2,3,1,0:T(1,128)S(1)} fusion(f32[2,9,12,128]{3,2,1,0:T(8,128)S(1)} %slice_bitcast_fusion.2, f32[2,4,9,128]{3,2,1,0:T(8,128)S(1)} %multiply_exponential_fusion.2, f32[2,9,128,1,1]{2,0,1,3,4:T(2,128)S(1)} %bitcast.308), kind=kOutput, calls=%fused_computation.17.clone.1 | convolution fusion | flops 1437696 | bytes 157056 | tf_op jit(solution)/shard_map/while/body/eval_jaxpr/rcpnko,rcno->rcpk/dot_general | solution.py:87
  93.3 2.1 %convolution_bitcast_fusion.9 = f32[12,2,1,2,2,8,2,8]{0,7,5,3,6,4,1,2:T(8,128)S(1)} fusion(f32[2,2,2,12,12,1,1]{4,3,6,5,2,1,0:T(8,128)S(1)} %bitcast.300, f32[12,2,2,2,8,2,8]{6,5,4,3,2,1,0:T(2,128)S(1)} %reshape.527), kind=kOutput, calls=%fused_computation.clone.1 | convolution fusion | flops 1769472 | bytes 102912 | tf_op jit(solution)/shard_map/while/body/eval_jaxpr/jrcvaybx,rcabjk->krcvaybx/dot_general | solution.py:105
  95.4 1.4 copy.115
  98.5 2.4 %convolution_bitcast_fusion.7 = f32[2,4,12,1]{2,3,1,0:T(1,128)S(1)} fusion(f32[2,9,12,128]{3,2,1,0:T(8,128)S(1)} %slice_bitcast_fusion.2, f32[2,4,9,128]{3,2,1,0:T(8,128)S(1)} %multiply_exponential_fusion.2, f32[2,9,128,1,1]{2,0,1,3,4:T(2,128)S(1)} %bitcast.308), kind=kOutput, calls=%fused_computation.17.clone.1 | convolution fusion | flops 1437696 | bytes 157056 | tf_op jit(solution)/shard_map/while/body/eval_jaxpr/rcpnko,rcno->rcpk/dot_general | solution.py:87
  107.0 2.1 %convolution_bitcast_fusion.9 = f32[12,2,1,2,2,8,2,8]{0,7,5,3,6,4,1,2:T(8,128)S(1)} fusion(f32[2,2,2,12,12,1,1]{4,3,6,5,2,1,0:T(8,128)S(1)} %bitcast.300, f32[12,2,2,2,8,2,8]{6,5,4,3,2,1,0:T(2,128)S(1)} %reshape.527), kind=kOutput, calls=%fused_computation.clone.1 | convolution fusion | flops 1769472 | bytes 102912 | tf_op jit(solution)/shard_map/while/body/eval_jaxpr/jrcvaybx,rcabjk->krcvaybx/dot_general | solution.py:105
  109.1 1.4 copy.115
  112.2 2.4 %convolution_bitcast_fusion.7 = f32[2,4,12,1]{2,3,1,0:T(1,128)S(1)} fusion(f32[2,9,12,128]{3,2,1,0:T(8,128)S(1)} %slice_bitcast_fusion.2, f32[2,4,9,128]{3,2,1,0:T(8,128)S(1)} %multiply_exponential_fusion.2, f32[2,9,128,1,1]{2,0,1,3,4:T(2,128)S(1)} %bitcast.308), kind=kOutput, calls=%fused_computation.17.clone.1 | convolution fusion | flops 1437696 | bytes 157056 | tf_op jit(solution)/shard_map/while/body/eval_jaxpr/rcpnko,rcno->rcpk/dot_general | solution.py:87
  120.7 2.1 %convolution_bitcast_fusion.9 = f32[12,2,1,2,2,8,2,8]{0,7,5,3,6,4,1,2:T(8,128)S(1)} fusion(f32[2,2,2,12,12,1,1]{4,3,6,5,2,1,0:T(8,128)S(1)} %bitcast.300, f32[12,2,2,2,8,2,8]{6,5,4,3,2,1,0:T(2,128)S(1)} %reshape.527), kind=kOutput, calls=%fused_computation.clone.1 | convolution fusion | flops 1769472 | bytes 102912 | tf_op jit(solution)/shard_map/while/body/eval_jaxpr/jrcvaybx,rcabjk->krcvaybx/dot_general | solution.py:105
  122.8 1.4 copy.115
  125.9 2.4 %convolution_bitcast_fusion.7 = f32[2,4,12,1]{2,3,1,0:T(1,128)S(1)} fusion(f32[2,9,12,128]{3,2,1,0:T(8,128)S(1)} %slice_bitcast_fusion.2, f32[2,4,9,128]{3,2,1,0:T(8,128)S(1)} %multiply_exponential_fusion.2, f32[2,9,128,1,1]{2,0,1,3,4:T(2,128)S(1)} %bitcast.308), kind=kOutput, calls=%fused_computation.17.clone.1 | convolution fusion | flops 1437696 | bytes 157056 | tf_op jit(solution)/shard_map/while/body/eval_jaxpr/rcpnko,rcno->rcpk/dot_general | solution.py:87
  134.4 2.1 %convolution_bitcast_fusion.9 = f32[12,2,1,2,2,8,2,8]{0,7,5,3,6,4,1,2:T(8,128)S(1)} fusion(f32[2,2,2,12,12,1,1]{4,3,6,5,2,1,0:T(8,128)S(1)} %bitcast.300, f32[12,2,2,2,8,2,8]{6,5,4,3,2,1,0:T(2,128)S(1)} %reshape.527), kind=kOutput, calls=%fused_computation.clone.1 | convolution fusion | flops 1769472 | bytes 102912 | tf_op jit(solution)/shard_map/while/body/eval_jaxpr/jrcvaybx,rcabjk->krcvaybx/dot_general | solution.py:105
  139.6 2.4 %convolution_bitcast_fusion.7 = f32[2,4,12,1]{2,3,1,0:T(1,128)S(1)} fusion(f32[2,9,12,128]{3,2,1,0:T(8,128)S(1)} %slice_bitcast_fusion.2, f32[2,4,9,128]{3,2,1,0:T(8,128)S(1)} %multiply_exponential_fusion.2, f32[2,9,128,1,1]{2,0,1,3,4:T(2,128)S(1)} %bitcast.308), kind=kOutput, calls=%fused_computation.17.clone.1 | convolution fusion | flops 1437696 | bytes 157056 | tf_op jit(solution)/shard_map/while/body/eval_jaxpr/rcpnko,rcno->rcpk/dot_general | solution.py:87
  148.1 2.1 %convolution_bitcast_fusion.9 = f32[12,2,1,2,2,8,2,8]{0,7,5,3,6,4,1,2:T(8,128)S(1)} fusion(f32[2,2,2,12,12,1,1]{4,3,6,5,2,1,0:T(8,128)S(1)} %bitcast.300, f32[12,2,2,2,8,2,8]{6,5,4,3,2,1,0:T(2,128)S(1)} %reshape.527), kind=kOutput, calls=%fused_computation.clone.1 | convolution fusion | flops 1769472 | bytes 102912 | tf_op jit(solution)/shard_map/while/body/eval_jaxpr/jrcvaybx,rcabjk->krcvaybx/dot_general | solution.py:105
  153.0 18.6 %all_to_all.30 = f32[32,3,2,1,512]{4,2,1,3,0:T(2,128)S(1)} all-to-all(f32[32,3,2,1,512]{4,2,1,3,0:T(2,128)S(1)} %bitcast.305), channel_id=1, replica_groups=mesh['member'=4,'region'=8] {'member','region'}, dimensions={0} | all-to-all | bytes 786432 | tf_op jit(solution)/shard_map/all_to_all | solution.py:149
  (421 shorter events, 65.9 us)
Async XLA Ops:
  0.0 9.4 %copy-start = (s32[16,1,128]{2,1,0:T(1,128)S(1)}, s32[16,1,128]{2,1,0:T(1,128)}, u32[]{:S(2)}) copy-start(s32[16,1,128]{2,1,0:T(1,128)} %param.10) | copy-start | bytes 24580
  2.1 20.8 %all-to-all-start = ((f32[1,3,2,32,512]{4,2,1,0,3:T(2,128)}), f32[1,3,2,32,512]{4,2,1,0,3:T(2,128)S(1)}, u32[]{:S(2)}, u32[]{:S(2)}) async-start(f32[1,3,2,32,512]{4,2,1,0,3:T(2,128)} %bitcast.189), calls=%async_computation | async-start | bytes 786432 | tf_op jit(solution)/shard_map/all_to_all | solution.py:117
  23.4 4.1 %copy-start.1 = (f32[16,1,128]{2,1,0:T(1,128)S(1)}, f32[16,1,128]{2,1,0:T(1,128)}, u32[]{:S(2)}) copy-start(f32[16,1,128]{2,1,0:T(1,128)} %param.9) | copy-start | bytes 24580
  23.4 4.1 %copy-start.2 = (f32[16,1,128]{2,1,0:T(1,128)S(1)}, f32[16,1,128]{2,1,0:T(1,128)}, u32[]{:S(2)}) copy-start(f32[16,1,128]{2,1,0:T(1,128)} %param.8) | copy-start | bytes 24580
  23.4 4.1 %copy-start.3 = (s32[16,1]{0,1:T(1,128)S(1)}, s32[16,1]{0,1:T(1,128)}, u32[]{:S(2)}) copy-start(s32[16,1]{0,1:T(1,128)} %param.11) | copy-start | bytes 196
  31.6 5.9 %collective-permute-start = (f32[16,1,15,128]{3,2,0,1:T(8,128)S(1)}, f32[16,1,15,128]{3,2,0,1:T(8,128)S(1)}, u32[]{:S(2)}, u32[]{:S(2)}) collective-permute-start(f32[16,1,15,128]{3,2,0,1:T(8,128)S(1)} %pad_maximum_fusion), channel_id=1, source_target_pairs={{0,1},{1,2},{2,3},{3,4},{4,5},{5,6},{6,7},{7,8},{8,9},{9,10},{10,1... | collective-permute-start | bytes 368648 | tf_op jit(solution)/shard_map/ppermute | solution.py:21
  34.5 8.5 %collective-permute-start.1 = (f32[16,1,15,128]{3,2,0,1:T(8,128)S(1)}, f32[16,1,15,128]{3,2,0,1:T(8,128)S(1)}, u32[]{:S(2)}, u32[]{:S(2)}) collective-permute-start(f32[16,1,15,128]{3,2,0,1:T(8,128)S(1)} %pad_maximum_fusion), channel_id=1, source_target_pairs={{1,0},{2,1},{3,2},{4,3},{5,4},{6,5},{7,6},{8,7},{9,8},{10,9},{11,1... | collective-permute-start | bytes 368648 | tf_op jit(solution)/shard_map/ppermute | solution.py:23
where the time goes:
time: 173 us; the launch traced here: 172 us
  matrix products  79.8 us (46%)
  local copies, waits for them, and re-layouts  35.4 us (20%)
  waiting for transfers between devices  20.1 us (12%)
  blocking collectives  18.6 us (11%)
  starting transfers between devices  11.7 us (7%)
  other arithmetic  3.63 us (2%)
  loops' own time  3.01 us (2%)
    dot_general x136, matrix products, batch_product(): jnp.einsum('...ij,...jk->...ik', left, right, precision=lax.Precision.HIG...  26.5 us
    dot_general x8, matrix products, analyze(): jnp.einsum('rcpnko,rcno->rcpk', weighted, innovation, precision=lax.Preci...  19 us
    all_to_all x1, blocking collectives, local(): lax.all_to_all(outgoing, ('member', 'region'), split_axis=0, concat_axis=...  18.6 us
    dot_general x8, matrix products, analyze(): jnp.einsum('jrcvaybx,rcabjk->krcvaybx', shaped, point_weights, precision=...  16.6 us
    all_to_all x1, waiting for transfers between devices, local(): lax.all_to_all(ensemble[None], ('member', 'region'), split_axis=3, concat...  13.4 us
    transpose x8, local copies, waits for them, and re-layouts, analyze(): jnp.einsum('jrcvaybx,rcabjk->krcvaybx', shaped, point_weights, precision=...  11.2 us
    another operation x8, local copies, waits for them, and re-layouts  9.76 us
    reshape x8, local copies, waits for them, and re-layouts, analyze(): return ens_mean[None] + updated.reshape(anomaly.shape)  9.01 us
  transfers between devices with their start and end apart: 3, of which 3 were waited for; matrix products, arithmetic and copies ran while one was open for 0% of the time, Pallas kernels for 0%

commit v1 on v0

--- a/solution.py
+++ b/solution.py
@@ -114,8 +114,14 @@
     values_len = ensemble.shape[3]
     member_count = lax.axis_size("member")
     region_count = lax.axis_size("region")
-    arrived = lax.all_to_all(
-        ensemble[None], ("member", "region"), split_axis=3, concat_axis=0, tiled=True
+    arrived = jnp.concatenate(
+        lax.all_to_all(
+            jnp.stack(jnp.split(ensemble[None], lax.axis_size(("member", "region")), axis=3)),
+            ("member", "region"),
+            0,
+            0,
+        ),
+        axis=0,
     )
     col_dev = arrived.shape[3]
     grouped = arrived.reshape(

time: 173 us -> 220 us (1.27)
  local copies, waits for them, and re-layouts: 35.4 us -> 81.6 us
    unnamed x9 -> x39, local copies, waits for them, and re-layouts: 2.09 us -> 46.6 us
    another operation x8 -> x10, local copies, waits for them, and re-layouts: 9.76 us -> 11.5 us
where the time goes in v1:
time: 220 us; the launch traced here: 219 us
  local copies, waits for them, and re-layouts  81.6 us (37%)
  matrix products  79.8 us (36%)
  waiting for transfers between devices  20.4 us (9%)
  blocking collectives  18.6 us (8%)
  starting transfers between devices  11.7 us (5%)
  other arithmetic  3.72 us (2%)
  loops' own time  3.01 us (1%)
    unnamed x39, local copies, waits for them, and re-layouts  46.6 us
    dot_general x136, matrix products, batch_product(): jnp.einsum('...ij,...jk->...ik', left, right, precision=lax.Precision.HIG...  26.5 us
    dot_general x8, matrix products, analyze(): jnp.einsum('rcpnko,rcno->rcpk', weighted, innovation, precision=lax.Preci...  19 us
    all_to_all x1, blocking collectives, local(): lax.all_to_all(outgoing, ('member', 'region'), split_axis=0, concat_axis=...  18.6 us
    dot_general x8, matrix products, analyze(): jnp.einsum('jrcvaybx,rcabjk->krcvaybx', shaped, point_weights, precision=...  16.6 us
    all_to_all x1, waiting for transfers between devices, local(): lax.all_to_all(jnp.stack(jnp.split(ensemble[None], lax.axis_size(('member...  13.4 us
    transpose x8, local copies, waits for them, and re-layouts, analyze(): jnp.einsum('jrcvaybx,rcabjk->krcvaybx', shaped, point_weights, precision=...  11.2 us
    another operation x8, local copies, waits for them, and re-layouts  9.76 us
  transfers between devices with their start and end apart: 3, of which 3 were waited for; matrix products, arithmetic and copies ran while one was open for 0% of the time, Pallas kernels for 0%

profile of v1, /device:TPU:0, one launch (start us, length us, event | category | flops | bytes accessed | tf_op | source)
XLA Modules:
  0.0 219.0 jit_solution(8128146561989934853)
XLA Ops:
  0.0 1.5 constant_dynamic-update-slice_fusion.40
  6.0 1.5 constant_dynamic-update-slice_fusion.36
  9.0 1.5 constant_dynamic-update-slice_fusion.34
  15.0 1.5 constant_dynamic-update-slice_fusion.30
  18.0 1.5 constant_dynamic-update-slice_fusion.28
  27.1 1.5 constant_dynamic-update-slice_fusion.22
  34.6 1.5 constant_dynamic-update-slice_fusion.17
  39.1 1.5 constant_dynamic-update-slice_fusion.14
  48.1 7.3 %all-to-all-start = ((f32[32,1,3,2,1,512]{5,4,3,2,1,0:T(1,128)}), f32[32,1,3,2,1,512]{5,4,3,2,1,0:T(1,128)S(1)}, u32[]{:S(2)}, u32[]{:S(2)}) async-start(f32[32,1,3,2,1,512]{5,4,3,2,1,0:T(1,128)} %constant_dynamic-update-slice_fusion.9), calls=%async_computation | async-start | bytes 786432 | tf_op jit(solution)/shard_map/all_to_all | solution.py:118
  55.5 13.4 %all-to-all-done = f32[32,1,3,2,1,512]{5,4,3,2,1,0:T(1,128)S(1)} async-done(((f32[32,1,3,2,1,512]{5,4,3,2,1,0:T(1,128)}), f32[32,1,3,2,1,512]{5,4,3,2,1,0:T(1,128)S(1)}, u32[]{:S(2)}, u32[]{:S(2)}) %all-to-all-start) | async-done | bytes 393248 | tf_op jit(solution)/shard_map/all_to_all | solution.py:118
  70.0 4.1 %fusion.36 = f32[16,1,128]{2,1,0:T(1,128)S(1)} fusion(f32[16,512,1]{1,2,0:T(1,128)S(1)} %reshape.519, s32[16,128]{1,0:T(8,128)S(1)} %bitcast.470), kind=kOutput, calls=%fused_computation.88 | convolution fusion | flops 14680064 | bytes 49152 | tf_op jit(solution)/shard_map/rcov,rcv->rco/dot_general | solution.py:44
  74.2 4.0 %fusion.49 = f32[16,1,12,128]{3,2,0,1:T(8,128)S(1)} fusion(s32[16,128]{1,0:T(8,128)S(1)} %bitcast.471, f32[12,16,512]{2,1,0:T(8,128)S(1)} %broadcast_subtract_fusion.1, f32[16,128]{1,0:T(8,128)S(1)} %get-tuple-element.195), kind=kOutput, calls=%fused_computation.100 | convolution fusion | flops 153116672 | bytes 507904 | tf_op jit(solution)/shard_map/rcov,krcv->rcko/dot_general | solution.py:43
  78.2 2.9 %collective-permute-start = (f32[16,1,15,128]{3,2,0,1:T(8,128)S(1)}, f32[16,1,15,128]{3,2,0,1:T(8,128)S(1)}, u32[]{:S(2)}, u32[]{:S(2)}) collective-permute-start(f32[16,1,15,128]{3,2,0,1:T(8,128)S(1)} %pad_maximum_fusion), channel_id=1, source_target_pairs={{0,1},{1,2},{2,3},{3,4},{4,5},{5,6},{6,7},{7,8},{8,9},{9,10},{10,1... | collective-permute-start | bytes 368648 | tf_op jit(solution)/shard_map/ppermute | solution.py:21
  84.1 5.5 %collective-permute-done.1 = f32[16,1,15,128]{3,2,0,1:T(8,128)S(1)} collective-permute-done((f32[16,1,15,128]{3,2,0,1:T(8,128)S(1)}, f32[16,1,15,128]{3,2,0,1:T(8,128)S(1)}, u32[]{:S(2)}, u32[]{:S(2)}) %collective-permute-start.1) | collective-permute-done | bytes 122912 | tf_op jit(solution)/shard_map/ppermute | solution.py:23
  89.7 109.6 %while.16 = (s32[]{:T(128)}, f32[12,16,1,512]{3,1,0,2:T(8,128)S(1)}, f32[16,1,512]{2,0,1:T(8,128)S(1)}, f32[18,3,15,128]{3,2,0,1:T(8,128)S(1)}, f32[12,16,1,512]...) while((s32[]{:T(128)}, ...), condition=%wide.region_3.4_spmd, body=%wide.region_1.3_spmd.sunk | while | flops 22196300 | bytes 2025700 | solution.py:147
  90.3 2.4 %convolution_bitcast_fusion.7 = f32[2,4,12,1]{2,3,1,0:T(1,128)S(1)} fusion(f32[2,9,12,128]{3,2,1,0:T(8,128)S(1)} %slice_bitcast_fusion.34, f32[2,4,9,128]{3,2,1,0:T(8,128)S(1)} %multiply_exponential_fusion.2, f32[2,9,128,1,1]{2,0,1,3,4:T(2,128)S(1)} %bitcast.462), kind=kOutput, calls=%fused_computation.17.clone.1 | convolution fusion | flops 1437696 | bytes 157056 | tf_op jit(solution)/shard_map/while/body/eval_jaxpr/rcpnko,rcno->rcpk/dot_general | solution.py:87
  98.7 2.1 convolution_bitcast_fusion.9
  104.0 2.4 %convolution_bitcast_fusion.7 = f32[2,4,12,1]{2,3,1,0:T(1,128)S(1)} fusion(f32[2,9,12,128]{3,2,1,0:T(8,128)S(1)} %slice_bitcast_fusion.34, f32[2,4,9,128]{3,2,1,0:T(8,128)S(1)} %multiply_exponential_fusion.2, f32[2,9,128,1,1]{2,0,1,3,4:T(2,128)S(1)} %bitcast.462), kind=kOutput, calls=%fused_computation.17.clone.1 | convolution fusion | flops 1437696 | bytes 157056 | tf_op jit(solution)/shard_map/while/body/eval_jaxpr/rcpnko,rcno->rcpk/dot_general | solution.py:87
  112.4 2.1 convolution_bitcast_fusion.9
  117.7 2.4 %convolution_bitcast_fusion.7 = f32[2,4,12,1]{2,3,1,0:T(1,128)S(1)} fusion(f32[2,9,12,128]{3,2,1,0:T(8,128)S(1)} %slice_bitcast_fusion.34, f32[2,4,9,128]{3,2,1,0:T(8,128)S(1)} %multiply_exponential_fusion.2, f32[2,9,128,1,1]{2,0,1,3,4:T(2,128)S(1)} %bitcast.462), kind=kOutput, calls=%fused_computation.17.clone.1 | convolution fusion | flops 1437696 | bytes 157056 | tf_op jit(solution)/shard_map/while/body/eval_jaxpr/rcpnko,rcno->rcpk/dot_general | solution.py:87
  126.1 2.1 convolution_bitcast_fusion.9
  131.4 2.4 %convolution_bitcast_fusion.7 = f32[2,4,12,1]{2,3,1,0:T(1,128)S(1)} fusion(f32[2,9,12,128]{3,2,1,0:T(8,128)S(1)} %slice_bitcast_fusion.34, f32[2,4,9,128]{3,2,1,0:T(8,128)S(1)} %multiply_exponential_fusion.2, f32[2,9,128,1,1]{2,0,1,3,4:T(2,128)S(1)} %bitcast.462), kind=kOutput, calls=%fused_computation.17.clone.1 | convolution fusion | flops 1437696 | bytes 157056 | tf_op jit(solution)/shard_map/while/body/eval_jaxpr/rcpnko,rcno->rcpk/dot_general | solution.py:87
  139.8 2.1 convolution_bitcast_fusion.9
  145.1 2.4 %convolution_bitcast_fusion.7 = f32[2,4,12,1]{2,3,1,0:T(1,128)S(1)} fusion(f32[2,9,12,128]{3,2,1,0:T(8,128)S(1)} %slice_bitcast_fusion.34, f32[2,4,9,128]{3,2,1,0:T(8,128)S(1)} %multiply_exponential_fusion.2, f32[2,9,128,1,1]{2,0,1,3,4:T(2,128)S(1)} %bitcast.462), kind=kOutput, calls=%fused_computation.17.clone.1 | convolution fusion | flops 1437696 | bytes 157056 | tf_op jit(solution)/shard_map/while/body/eval_jaxpr/rcpnko,rcno->rcpk/dot_general | solution.py:87
  153.5 2.1 convolution_bitcast_fusion.9
  158.8 2.4 %convolution_bitcast_fusion.7 = f32[2,4,12,1]{2,3,1,0:T(1,128)S(1)} fusion(f32[2,9,12,128]{3,2,1,0:T(8,128)S(1)} %slice_bitcast_fusion.34, f32[2,4,9,128]{3,2,1,0:T(8,128)S(1)} %multiply_exponential_fusion.2, f32[2,9,128,1,1]{2,0,1,3,4:T(2,128)S(1)} %bitcast.462), kind=kOutput, calls=%fused_computation.17.clone.1 | convolution fusion | flops 1437696 | bytes 157056 | tf_op jit(solution)/shard_map/while/body/eval_jaxpr/rcpnko,rcno->rcpk/dot_general | solution.py:87
  167.2 2.1 convolution_bitcast_fusion.9
  172.5 2.4 %convolution_bitcast_fusion.7 = f32[2,4,12,1]{2,3,1,0:T(1,128)S(1)} fusion(f32[2,9,12,128]{3,2,1,0:T(8,128)S(1)} %slice_bitcast_fusion.34, f32[2,4,9,128]{3,2,1,0:T(8,128)S(1)} %multiply_exponential_fusion.2, f32[2,9,128,1,1]{2,0,1,3,4:T(2,128)S(1)} %bitcast.462), kind=kOutput, calls=%fused_computation.17.clone.1 | convolution fusion | flops 1437696 | bytes 157056 | tf_op jit(solution)/shard_map/while/body/eval_jaxpr/rcpnko,rcno->rcpk/dot_general | solution.py:87
  180.9 2.1 convolution_bitcast_fusion.9
  186.2 2.4 %convolution_bitcast_fusion.7 = f32[2,4,12,1]{2,3,1,0:T(1,128)S(1)} fusion(f32[2,9,12,128]{3,2,1,0:T(8,128)S(1)} %slice_bitcast_fusion.34, f32[2,4,9,128]{3,2,1,0:T(8,128)S(1)} %multiply_exponential_fusion.2, f32[2,9,128,1,1]{2,0,1,3,4:T(2,128)S(1)} %bitcast.462), kind=kOutput, calls=%fused_computation.17.clone.1 | convolution fusion | flops 1437696 | bytes 157056 | tf_op jit(solution)/shard_map/while/body/eval_jaxpr/rcpnko,rcno->rcpk/dot_general | solution.py:87
  194.6 2.1 convolution_bitcast_fusion.9
  199.6 18.6 %all_to_all.20 = f32[32,3,2,1,512]{4,2,1,3,0:T(2,128)S(1)} all-to-all(f32[32,3,2,1,512]{4,2,1,3,0:T(2,128)S(1)} %bitcast.427), channel_id=1, replica_groups=mesh['member'=4,'region'=8] {'member','region'}, dimensions={0} | all-to-all | bytes 786432 | tf_op jit(solution)/shard_map/all_to_all | solution.py:155
  (452 shorter events, 112.4 us)
Async XLA Ops:
  0.0 55.4 %copy-start = (s32[16,1,128]{2,1,0:T(1,128)S(1)}, s32[16,1,128]{2,1,0:T(1,128)}, u32[]{:S(2)}) copy-start(s32[16,1,128]{2,1,0:T(1,128)} %param.10) | copy-start | bytes 24580
  48.1 20.8 %all-to-all-start = ((f32[32,1,3,2,1,512]{5,4,3,2,1,0:T(1,128)}), f32[32,1,3,2,1,512]{5,4,3,2,1,0:T(1,128)S(1)}, u32[]{:S(2)}, u32[]{:S(2)}) async-start(f32[32,1,3,2,1,512]{5,4,3,2,1,0:T(1,128)} %constant_dynamic-update-slice_fusion.9), calls=%async_computation | async-start | bytes 786432 | tf_op jit(solution)/shard_map/all_to_all | solution.py:118
  70.0 4.1 %copy-start.1 = (f32[16,1,128]{2,1,0:T(1,128)S(1)}, f32[16,1,128]{2,1,0:T(1,128)}, u32[]{:S(2)}) copy-start(f32[16,1,128]{2,1,0:T(1,128)} %param.9) | copy-start | bytes 24580
  70.0 4.1 %copy-start.2 = (f32[16,1,128]{2,1,0:T(1,128)S(1)}, f32[16,1,128]{2,1,0:T(1,128)}, u32[]{:S(2)}) copy-start(f32[16,1,128]{2,1,0:T(1,128)} %param.8) | copy-start | bytes 24580
  70.0 4.1 %copy-start.3 = (s32[16,1]{0,1:T(1,128)S(1)}, s32[16,1]{0,1:T(1,128)}, u32[]{:S(2)}) copy-start(s32[16,1]{0,1:T(1,128)} %param.11) | copy-start | bytes 196
  78.2 5.9 %collective-permute-start = (f32[16,1,15,128]{3,2,0,1:T(8,128)S(1)}, f32[16,1,15,128]{3,2,0,1:T(8,128)S(1)}, u32[]{:S(2)}, u32[]{:S(2)}) collective-permute-start(f32[16,1,15,128]{3,2,0,1:T(8,128)S(1)} %pad_maximum_fusion), channel_id=1, source_target_pairs={{0,1},{1,2},{2,3},{3,4},{4,5},{5,6},{6,7},{7,8},{8,9},{9,10},{10,1... | collective-permute-start | bytes 368648 | tf_op jit(solution)/shard_map/ppermute | solution.py:21
  81.1 8.5 %collective-permute-start.1 = (f32[16,1,15,128]{3,2,0,1:T(8,128)S(1)}, f32[16,1,15,128]{3,2,0,1:T(8,128)S(1)}, u32[]{:S(2)}, u32[]{:S(2)}) collective-permute-start(f32[16,1,15,128]{3,2,0,1:T(8,128)S(1)} %pad_maximum_fusion), channel_id=1, source_target_pairs={{1,0},{2,1},{3,2},{4,3},{5,4},{6,5},{7,6},{8,7},{9,8},{10,9},{11,1... | collective-permute-start | bytes 368648 | tf_op jit(solution)/shard_map/ppermute | solution.py:23
